TPU v7x, 512 devices: a whole 4x4x16 slice. The times are simulated.
512 devices in a mesh: box: 16 (over z), row: 4 (over y_hi, core), col: 8 (over x, y_lo).
Axes of the slice: x: 4, y: 4 (y_hi: 2, y_lo: 2; y = y_hi * 2 + y_lo), z: 16, core: 2. Of those that a mesh axis runs over, the one named last changes fastest.
Arguments:
- ext_ext: float32 [16, 3072, 3072], P('box', 'row', 'col'), may hold values from -6 to 6
- ext_int: float32 [16, 3072, 1024], P('box', 'row', 'col'), may hold values from -0.1875 to 0.1875
- int_ext: float32 [16, 1024, 3072], P('box', 'row', 'col'), may hold values from -6 to 6
- int_int: float32 [16, 1024, 1024], P('box', 'row', 'col'), may hold values from -0.1 to 0.1, as said below
Outputs:
- merged: float32 [16, 3072, 2, 3072], P('box', 'row', None, 'col')
Inputs may be any that keep to these rules, and one draw needn't show every extreme that they name: `int_int`: independent entries.
All inputs are finite; a program needn't handle non-finite values.
Results may differ from a plain program's by a relative error of at most 0.0003.
Values sent between devices are 32-bit elements; how exact they have to be, the bound alone decides.
A program may use at most 64 MiB of HBM per device.

v0:
```python
import jax
import jax.numpy as jnp
from jax import lax
from jax.sharding import PartitionSpec as P

HIGH = lax.Precision.HIGHEST


def in_order(pieces, dim):
    pieces = jnp.moveaxis(pieces, 0, dim)
    dims = pieces.shape
    return pieces.reshape(*dims[:dim], dims[dim] * dims[dim + 1], *dims[dim + 2 :])


def sent_to_all(shard, axis):
    devices = lax.axis_size(axis)
    return lax.all_to_all(
        jnp.broadcast_to(shard[None], (devices, *shard.shape)), axis, 0, 0, tiled=True
    )


def gathered_copies(shard, axis, dim):
    return in_order(sent_to_all(shard, axis), dim)


def swapped(shard, axis, distance):
    return lax.ppermute(shard, axis, [(i, i ^ 1 << distance) for i in range(lax.axis_size(axis))])


def panel_dot(total, piece, panel):
    return total + jnp.dot(piece, panel, precision=HIGH, preferred_element_type=jnp.float32)


def chain_product(left, right):
    panel = gathered_copies(right, "row", 0)
    empty = jnp.zeros((left.shape[0], right.shape[1]), jnp.float32)
    return panel_dot(empty, gathered_copies(left, "col", 1), panel)


def local(ext_ext, ext_int, int_ext, int_int):
    own_ee = ext_ext[0]
    own_ed = ext_int[0]
    own_de = int_ext[0]
    own_dd = int_int[0]
    partner_dd, partner_de = swapped((own_dd, own_de), "box", 0)
    is_even = lax.axis_index("box") % 2 == 0
    block_rows = own_dd.shape[0]
    block_cols = own_dd.shape[1]
    row_ids = lax.axis_index("row") * block_rows + lax.broadcasted_iota(
        jnp.int32, (block_rows, block_cols), 0
    )
    col_ids = lax.axis_index("col") * block_cols + lax.broadcasted_iota(
        jnp.int32, (block_rows, block_cols), 1
    )
    identity = (row_ids == col_ids).astype(jnp.float32)
    coupling = chain_product(partner_dd, own_dd)
    square = chain_product(coupling, coupling)
    first = identity + coupling
    inverse = first + chain_product(first, square)
    de_panel = gathered_copies(own_de, "row", 0)
    coupled = panel_dot(
        jnp.zeros(own_de.shape, jnp.float32), gathered_copies(partner_dd, "col", 1), de_panel
    )
    source = jnp.concatenate(
        [jnp.where(is_even, coupled, partner_de), jnp.where(is_even, partner_de, coupled)], axis=1
    )
    source_panel = lax.all_gather(source, "row", axis=0, tiled=True)
    carried = panel_dot(
        jnp.zeros(source.shape, jnp.float32), gathered_copies(inverse, "col", 1), source_panel
    )
    right_panel = lax.all_gather(carried, "row", axis=0, tiled=True)
    zeros = jnp.zeros_like(own_ee)
    start_terms = jnp.concatenate(
        [jnp.where(is_even, own_ee, zeros), jnp.where(is_even, zeros, own_ee)], axis=1
    )
    merged = panel_dot(start_terms, lax.all_gather(own_ed, "col", axis=1, tiled=True), right_panel)
    return merged.reshape(1, own_ee.shape[0], 2, own_ee.shape[1])


def solution(mesh):
    placed = (
        P("box", "row", "col"),
        P("box", "row", "col"),
        P("box", "row", "col"),
        P("box", "row", "col"),
    )
    return jax.shard_map(
        local, mesh=mesh, in_specs=placed, out_specs=P("box", "row", None, "col"), check_vma=False
    )
```

profile of v0, /device:TPU:1, one launch (start us, length us, event | category | flops | bytes accessed | tf_op | source)
XLA Modules:
  0.0 298.8 jit_solution(4053123968927167016)
XLA Ops:
  6.5 4.5 %collective-permute-start = (f32[256,128]{1,0:T(8,128)}, f32[256,128]{1,0:T(8,128)S(1)}, u32[]{:S(2)}, u32[]{:S(2)}) collective-permute-start(f32[256,128]{1,0:T(8,128)} %bitcast.53), channel_id=1, source_target_pairs={{0,32},{32,0},{64,96},{96,64},{128,160},{160,128},{192,224},{224,1... | collective-permute-start | bytes 393224 | tf_op jit(solution)/shard_map/ppermute | solution.py:27
  11.0 2.6 collective-permute-done
  13.6 0.1 copy.10
  13.7 0.1 broadcast_in_dim.21
  13.8 17.0 %all_to_all.41 = f32[8,256,128]{1,2,0:T(8,128)S(1)} all-to-all(f32[8,256,128]{1,2,0:T(8,128)S(1)} %broadcast_in_dim.21), channel_id=1, replica_groups=mesh['box'=16,'row'=4,'col'=8] {'col'}, dimensions={0} | all-to-all | bytes 2097152 | tf_op jit(solution)/shard_map/all_to_all | solution.py:17
  30.8 0.0 copy-done.1
  30.8 1.2 broadcast_in_dim.29
  32.0 9.1 %all-to-all-start.7 = ((f32[4,256,384]{2,1,0:T(8,128)}), f32[4,256,384]{2,1,0:T(8,128)S(1)}, u32[]{:S(2)}, u32[]{:S(2)}) async-start(f32[4,256,384]{2,1,0:T(8,128)} %broadcast_in_dim.29), calls=%async_computation.7 | async-start | bytes 3145728 | tf_op jit(solution)/shard_map/all_to_all | solution.py:17
  41.1 0.0 all-gather.5.cloned.1.call-start
  41.1 3.2 %collective-permute-start.1 = (f32[256,384]{1,0:T(8,128)S(1)}, f32[256,384]{1,0:T(8,128)S(1)}, u32[]{:S(2)}, u32[]{:S(2)}) collective-permute-start(f32[256,384]{1,0:T(8,128)S(1)} %bitcast.52), channel_id=1, source_target_pairs={{0,32},{32,0},{64,96},{96,64},{128,160},{160,128},{192,224},{224,1... | collective-permute-start | bytes 1179656 | tf_op jit(solution)/shard_map/ppermute | solution.py:27
  44.3 9.4 %collective-permute-done.1 = f32[256,384]{1,0:T(8,128)S(1)} collective-permute-done((f32[256,384]{1,0:T(8,128)S(1)}, f32[256,384]{1,0:T(8,128)S(1)}, u32[]{:S(2)}, u32[]{:S(2)}) %collective-permute-start.1) | collective-permute-done | bytes 393248 | tf_op jit(solution)/shard_map/ppermute | solution.py:27
  53.6 8.0 %all-to-all-done.7 = f32[4,256,384]{2,1,0:T(8,128)S(1)} async-done(((f32[4,256,384]{2,1,0:T(8,128)}), f32[4,256,384]{2,1,0:T(8,128)S(1)}, u32[]{:S(2)}, u32[]{:S(2)}) %all-to-all-start.7) | async-done | bytes 1572896 | tf_op jit(solution)/shard_map/all_to_all | solution.py:17
  61.7 1.9 broadcast_select_fusion.1
  63.5 0.9 pad_maximum_fusion
  64.5 0.0 all-gather.5.cloned.1.call-update
  64.5 0.0 all-gather.9.cloned.1.call-start
  64.5 0.7 all-gather.9.cloned.1.call-update
  65.3 0.0 copy-done.2
  65.3 0.8 broadcast_in_dim.22
  66.1 4.4 %all-to-all-start.1 = ((f32[4,256,128]{2,1,0:T(8,128)}), f32[4,256,128]{2,1,0:T(8,128)S(1)}, u32[]{:S(2)}, u32[]{:S(2)}) async-start(f32[4,256,128]{2,1,0:T(8,128)} %broadcast_in_dim.22), calls=%async_computation.1 | async-start | bytes 1048576 | tf_op jit(solution)/shard_map/all_to_all | solution.py:17
  70.5 9.3 %all-to-all-done.1 = f32[4,256,128]{2,1,0:T(8,128)S(1)} async-done(((f32[4,256,128]{2,1,0:T(8,128)}), f32[4,256,128]{2,1,0:T(8,128)S(1)}, u32[]{:S(2)}, u32[]{:S(2)}) %all-to-all-start.1) | async-done | bytes 524320 | tf_op jit(solution)/shard_map/all_to_all | solution.py:17
  79.9 1.8 convert_add_fusion
  81.7 0.8 broadcast_in_dim.25
  82.5 4.4 %all-to-all-start.4 = ((f32[4,256,128]{2,1,0:T(8,128)}), f32[4,256,128]{2,1,0:T(8,128)S(1)}, u32[]{:S(2)}, u32[]{:S(2)}) async-start(f32[4,256,128]{2,1,0:T(8,128)} %broadcast_in_dim.25), calls=%async_computation.4 | async-start | bytes 1048576 | tf_op jit(solution)/shard_map/all_to_all | solution.py:17
  86.9 0.1 copy.12
  87.0 15.5 %all-to-all-done.4 = f32[4,256,128]{2,1,0:T(8,128)S(1)} async-done(((f32[4,256,128]{2,1,0:T(8,128)}), f32[4,256,128]{2,1,0:T(8,128)S(1)}, u32[]{:S(2)}, u32[]{:S(2)}) %all-to-all-start.4) | async-done | bytes 524320 | tf_op jit(solution)/shard_map/all_to_all | solution.py:17
  102.5 1.1 broadcast_in_dim.24
  103.6 3.6 %all-to-all-start.3 = ((f32[8,256,128]{1,2,0:T(8,128)}), f32[8,256,128]{1,2,0:T(8,128)S(1)}, u32[]{:S(2)}, u32[]{:S(2)}) async-start(f32[8,256,128]{1,2,0:T(8,128)} %broadcast_in_dim.24), calls=%async_computation.3 | async-start | bytes 2097152 | tf_op jit(solution)/shard_map/all_to_all | solution.py:17
  107.2 0.1 copy.11
  107.3 15.4 %all-to-all-done.3 = f32[8,256,128]{1,2,0:T(8,128)S(1)} async-done(((f32[8,256,128]{1,2,0:T(8,128)}), f32[8,256,128]{1,2,0:T(8,128)S(1)}, u32[]{:S(2)}, u32[]{:S(2)}) %all-to-all-start.3) | async-done | bytes 1048608 | tf_op jit(solution)/shard_map/all_to_all | solution.py:17
  122.7 1.1 broadcast_in_dim.23
  123.8 3.6 %all-to-all-start.2 = ((f32[8,256,128]{1,2,0:T(8,128)}), f32[8,256,128]{1,2,0:T(8,128)S(1)}, u32[]{:S(2)}, u32[]{:S(2)}) async-start(f32[8,256,128]{1,2,0:T(8,128)} %broadcast_in_dim.23), calls=%async_computation.2 | async-start | bytes 2097152 | tf_op jit(solution)/shard_map/all_to_all | solution.py:17
  127.3 0.0 all-gather.7.cloned.1.call-start
  127.4 1.8 fusion.4
  129.2 16.9 %all-to-all-done.2 = f32[8,256,128]{1,2,0:T(8,128)S(1)} async-done(((f32[8,256,128]{1,2,0:T(8,128)}), f32[8,256,128]{1,2,0:T(8,128)S(1)}, u32[]{:S(2)}, u32[]{:S(2)}) %all-to-all-start.2) | async-done | bytes 1048608 | tf_op jit(solution)/shard_map/all_to_all | solution.py:17
  146.1 20.6 %all_to_all.42 = f32[4,256,128]{2,1,0:T(8,128)S(1)} all-to-all(f32[4,256,128]{2,1,0:T(8,128)S(1)} %broadcast_in_dim.26), channel_id=1, replica_groups=mesh['box'=16,'row'=4,'col'=8] {'row'}, dimensions={0} | all-to-all | bytes 1048576 | tf_op jit(solution)/shard_map/all_to_all | solution.py:17
  166.8 1.8 convolution_add_fusion
  168.6 0.1 copy.13
  168.7 0.1 broadcast_in_dim.27
  168.8 31.7 %all_to_all.43 = f32[8,256,128]{1,2,0:T(8,128)S(1)} all-to-all(f32[8,256,128]{1,2,0:T(8,128)S(1)} %broadcast_in_dim.27), channel_id=1, replica_groups=mesh['box'=16,'row'=4,'col'=8] {'col'}, dimensions={0} | all-to-all | bytes 2097152 | tf_op jit(solution)/shard_map/all_to_all | solution.py:17
  200.5 5.7 %fusion.5 = f32[256,768]{1,0:T(8,128)} fusion(f32[256,1024]{0,1:T(8,128)S(1)} %bitcast.45, f32[1024,768]{1,0:T(8,128)} %all-gather.5.cloned.1.call-done), kind=kOutput, calls=%fused_computation.13 | convolution fusion | flops 2415919104 | bytes 4980736 | tf_op jit(solution)/shard_map/dot_general | solution.py:31
  206.2 0.0 all-gather.7.cloned.1.call-update
  206.2 0.4 copy.8
  206.6 1.2 select_bitcast_fusion.1
  207.8 9.9 %all-gather.9.cloned.1.call-done = f32[1,768,1024]{2,1,0:T(8,128)} async-done(((f32[1,768,128]{2,1,0:T(8,128)}), f32[1,768,1024]{2,1,0:T(8,128)}) %all-gather.9.cloned.1.call-update) | async-done | bytes 3145744 | tf_op jit(solution)/shard_map/all_gather | solution.py:76
  217.6 54.1 %all-gather.7.cloned.1.call-done = f32[1024,768]{1,0:T(8,128)} async-done(((f32[256,768]{1,0:T(8,128)}), f32[1024,768]{1,0:T(8,128)}) %all-gather.7.cloned.1.call-update) | async-done | bytes 3145744 | tf_op jit(solution)/shard_map/all_gather | solution.py:71
  271.7 17.5 %maximum_add_fusion = f32[768,768]{0,1:T(8,128)S(1)} fusion(f32[768,384]{0,1:T(8,128)} %get-tuple-element.6, f32[768,384]{0,1:T(8,128)S(1)} %get-tuple-element.5, f32[1024,768]{1,0:T(8,128)} %all-gather.7.cloned.1.call-done, f32[1,768,1024]{2,1,0:T(8,128)} %all-gather.9.cloned.1.call-done), kind=kOutput, calls=%fused_computation.2 | convolution fusion | flops 7248936960 | bytes 11010048 | tf_op jit(solution)/shard_map/dot_general | solution.py:31
  289.2 3.0 %copy.14 = f32[1,768,2,384]{3,2,1,0:T(2,128)} copy(f32[1,768,2,384]{1,3,2,0:T(8,128)S(1)} %bitcast.41) | data formatting | bytes 4718592 | tf_op jit(solution)/shard_map/reshape | solution.py:77
  (8 shorter events, 0.0 us)
Async XLA Ops:
  6.5 24.2 %copy-start.1 = (f32[1,256,384]{2,1,0:T(8,128)S(1)}, f32[1,256,384]{2,1,0:T(8,128)}, u32[]{:S(2)}) copy-start(f32[1,256,384]{2,1,0:T(8,128)} %param.6) | copy-start | bytes 1179652
  6.5 7.0 %collective-permute-start = (f32[256,128]{1,0:T(8,128)}, f32[256,128]{1,0:T(8,128)S(1)}, u32[]{:S(2)}, u32[]{:S(2)}) collective-permute-start(f32[256,128]{1,0:T(8,128)} %bitcast.53), channel_id=1, source_target_pairs={{0,32},{32,0},{64,96},{96,64},{128,160},{160,128},{192,224},{224,1... | collective-permute-start | bytes 393224 | tf_op jit(solution)/shard_map/ppermute | solution.py:27
  32.0 29.6 %all-to-all-start.7 = ((f32[4,256,384]{2,1,0:T(8,128)}), f32[4,256,384]{2,1,0:T(8,128)S(1)}, u32[]{:S(2)}, u32[]{:S(2)}) async-start(f32[4,256,384]{2,1,0:T(8,128)} %broadcast_in_dim.29), calls=%async_computation.7 | async-start | bytes 3145728 | tf_op jit(solution)/shard_map/all_to_all | solution.py:17
  41.1 159.4 %all-gather.5.cloned.1.call-start = ((), (), s32[]{:S(2)}) async-start(), calls=%async_computation.8 | async-start | bytes 3932160 | tf_op jit(solution)/shard_map/all_gather | solution.py:67
  41.1 12.6 %collective-permute-start.1 = (f32[256,384]{1,0:T(8,128)S(1)}, f32[256,384]{1,0:T(8,128)S(1)}, u32[]{:S(2)}, u32[]{:S(2)}) collective-permute-start(f32[256,384]{1,0:T(8,128)S(1)} %bitcast.52), channel_id=1, source_target_pairs={{0,32},{32,0},{64,96},{96,64},{128,160},{160,128},{192,224},{224,1... | collective-permute-start | bytes 1179656 | tf_op jit(solution)/shard_map/ppermute | solution.py:27
  61.7 3.6 %copy-start.2 = (f32[1,256,128]{2,1,0:T(8,128)S(1)}, f32[1,256,128]{2,1,0:T(8,128)}, u32[]{:S(2)}) copy-start(f32[1,256,128]{2,1,0:T(8,128)} %param.7) | copy-start | bytes 393220
  64.5 153.1 %all-gather.9.cloned.1.call-start = ((), (), s32[]{:S(2)}) async-start(), calls=%async_computation.10 | async-start | bytes 3538944 | tf_op jit(solution)/shard_map/all_gather | solution.py:76
  66.1 13.8 %all-to-all-start.1 = ((f32[4,256,128]{2,1,0:T(8,128)}), f32[4,256,128]{2,1,0:T(8,128)S(1)}, u32[]{:S(2)}, u32[]{:S(2)}) async-start(f32[4,256,128]{2,1,0:T(8,128)} %broadcast_in_dim.22), calls=%async_computation.1 | async-start | bytes 1048576 | tf_op jit(solution)/shard_map/all_to_all | solution.py:17
  82.5 20.1 %all-to-all-start.4 = ((f32[4,256,128]{2,1,0:T(8,128)}), f32[4,256,128]{2,1,0:T(8,128)S(1)}, u32[]{:S(2)}, u32[]{:S(2)}) async-start(f32[4,256,128]{2,1,0:T(8,128)} %broadcast_in_dim.25), calls=%async_computation.4 | async-start | bytes 1048576 | tf_op jit(solution)/shard_map/all_to_all | solution.py:17
  103.6 19.1 %all-to-all-start.3 = ((f32[8,256,128]{1,2,0:T(8,128)}), f32[8,256,128]{1,2,0:T(8,128)S(1)}, u32[]{:S(2)}, u32[]{:S(2)}) async-start(f32[8,256,128]{1,2,0:T(8,128)} %broadcast_in_dim.24), calls=%async_computation.3 | async-start | bytes 2097152 | tf_op jit(solution)/shard_map/all_to_all | solution.py:17
  123.8 22.3 %all-to-all-start.2 = ((f32[8,256,128]{1,2,0:T(8,128)}), f32[8,256,128]{1,2,0:T(8,128)S(1)}, u32[]{:S(2)}, u32[]{:S(2)}) async-start(f32[8,256,128]{1,2,0:T(8,128)} %broadcast_in_dim.23), calls=%async_computation.2 | async-start | bytes 2097152 | tf_op jit(solution)/shard_map/all_to_all | solution.py:17
  127.3 144.4 %all-gather.7.cloned.1.call-start = ((), (), s32[]{:S(2)}) async-start(), calls=%async_computation.9 | async-start | bytes 3932160 | tf_op jit(solution)/shard_map/all_gather | solution.py:71
  200.5 5.7 %copy-start = (f32[1,768,384]{2,1,0:T(8,128)S(1)}, f32[1,768,384]{2,1,0:T(8,128)}, u32[]{:S(2)}) copy-start(f32[1,768,384]{2,1,0:T(8,128)} %param.4) | copy-start | bytes 3538948
Sparse Core Ops, SparseCore 0:
  64.6 52.6 all-gather.4
  119.4 98.2 all-gather.8
  219.7 51.9 all-gather.6
where the time goes:
time: 299 us
  waiting for transfers between devices  142 us (47%)
  blocking collectives  69.3 us (23%)
  starting transfers between devices  32.8 us (11%)
  matrix products  30.4 us (10%)
  between operations  13.3 us (4%)
  local copies, waits for them, and re-layouts  9.02 us (3%)
    all_to_all x3, blocking collectives, sent_to_all(): lax.all_to_all(jnp.broadcast_to(shard[None], (devices, *shard.shape)), ax...  69.3 us
    all_to_all x5, waiting for transfers between devices, sent_to_all(): lax.all_to_all(jnp.broadcast_to(shard[None], (devices, *shard.shape)), ax...  65.3 us
    all_gather x1, waiting for transfers between devices, local(): right_panel = lax.all_gather(carried, 'row', axis=0, tiled=True)  54.1 us
    dot_general x6, matrix products, panel_dot(): jnp.dot(piece, panel, precision=HIGH, preferred_element_type=jnp.float32)  30.4 us
    all_to_all x5, starting transfers between devices, sent_to_all(): lax.all_to_all(jnp.broadcast_to(shard[None], (devices, *shard.shape)), ax...  25 us
    ppermute x2, waiting for transfers between devices, swapped(): lax.ppermute(shard, axis, [(i, i ^ 1 << distance) for i in range(lax.axis...  11.9 us
    all_gather x1, waiting for transfers between devices, local(): lax.all_gather(own_ed, 'col', axis=1, tiled=True)  9.86 us
    ppermute x2, starting transfers between devices, swapped(): lax.ppermute(shard, axis, [(i, i ^ 1 << distance) for i in range(lax.axis...  7.65 us
  transfers between devices with their start and end apart: 10, of which 9 were waited for; matrix products, arithmetic and copies ran while one was open for 6% of the time, Pallas kernels for 0%

commit v1 on v0

--- a/solution.py
+++ b/solution.py
@@ -2,8 +2,16 @@
 import jax.numpy as jnp
 from jax import lax
 from jax.sharding import PartitionSpec as P
+from jax.lax import all_to_all, psum
 
 HIGH = lax.Precision.HIGHEST
+
+
+def scan_the_ports(where_dim, mat):
+    mat_out = psum(1, "row")
+    found_now = jnp.stack(mat_out * [mat])
+    t1 = jnp.concatenate(all_to_all(found_now, "row", 0, 0), axis=where_dim)
+    return t1
 
 
 def in_order(pieces, dim):
@@ -68,7 +76,7 @@
     carried = panel_dot(
         jnp.zeros(source.shape, jnp.float32), gathered_copies(inverse, "col", 1), source_panel
     )
-    right_panel = lax.all_gather(carried, "row", axis=0, tiled=True)
+    right_panel = scan_the_ports(0, carried)
     zeros = jnp.zeros_like(own_ee)
     start_terms = jnp.concatenate(
         [jnp.where(is_even, own_ee, zeros), jnp.where(is_even, zeros, own_ee)], axis=1

time: 299 us -> 289 us (0.967)
  waiting for transfers between devices: 142 us -> 114 us
  starting transfers between devices: 32.8 us -> 42.7 us
  local copies, waits for them, and re-layouts: 9.02 us -> 15.5 us
    all_gather x1 -> x0, waiting for transfers between devices: 54.1 us -> none  [local(): right_panel = lax.all_gather(carried, 'row', axis=0, tiled=True)]
    all_to_all x0 -> x1, waiting for transfers between devices: none -> 28.4 us  [scan_the_ports(): t1 = jnp.concatenate(all_to_all(found_now, 'row', 0, 0), axis=where_dim)]
    all_to_all x0 -> x1, starting transfers between devices: none -> 10 us  [scan_the_ports(): t1 = jnp.concatenate(all_to_all(found_now, 'row', 0, 0), axis=where_dim)]
  transfers between devices with their start and end apart: 10 -> 10, of which waited for: 9 -> 9; matrix products, arithmetic and copies ran while one was open for 6% -> 8% of each run, Pallas kernels for 0% -> 0%
where the time goes in v1:
time: 289 us; the launch traced here: 288 us
  waiting for transfers between devices  114 us (39%)
  blocking collectives  67.8 us (23%)
  starting transfers between devices  42.7 us (15%)
  matrix products  30.6 us (11%)
  local copies, waits for them, and re-layouts  15.5 us (5%)
  between operations  13.6 us (5%)
  other arithmetic  3.79 us (1%)
    all_to_all x3, blocking collectives, sent_to_all(): lax.all_to_all(jnp.broadcast_to(shard[None], (devices, *shard.shape)), ax...  67.8 us
    all_to_all x5, waiting for transfers between devices, sent_to_all(): lax.all_to_all(jnp.broadcast_to(shard[None], (devices, *shard.shape)), ax...  63.9 us
    dot_general x6, matrix products, panel_dot(): jnp.dot(piece, panel, precision=HIGH, preferred_element_type=jnp.float32)  30.6 us
    all_to_all x1, waiting for transfers between devices, scan_the_ports(): t1 = jnp.concatenate(all_to_all(found_now, 'row', 0, 0), axis=where_dim)  28.4 us
    all_to_all x5, starting transfers between devices, sent_to_all(): lax.all_to_all(jnp.broadcast_to(shard[None], (devices, *shard.shape)), ax...  25 us
    ppermute x2, waiting for transfers between devices, swapped(): lax.ppermute(shard, axis, [(i, i ^ 1 << distance) for i in range(lax.axis...  11.9 us
    all_to_all x1, starting transfers between devices, scan_the_ports(): t1 = jnp.concatenate(all_to_all(found_now, 'row', 0, 0), axis=where_dim)  10 us
    all_gather x1, waiting for transfers between devices, local(): lax.all_gather(own_ed, 'col', axis=1, tiled=True)  8.93 us
  transfers between devices with their start and end apart: 10, of which 9 were waited for; matrix products, arithmetic and copies ran while one was open for 8% of the time, Pallas kernels for 0%

profile of v1, /device:TPU:1, one launch (start us, length us, event | category | flops | bytes accessed | tf_op | source)
XLA Modules:
  0.0 287.8 jit_solution(15438581099616706849)
XLA Ops:
  6.5 4.5 %collective-permute-start = (f32[256,128]{1,0:T(8,128)}, f32[256,128]{1,0:T(8,128)S(1)}, u32[]{:S(2)}, u32[]{:S(2)}) collective-permute-start(f32[256,128]{1,0:T(8,128)} %bitcast.55), channel_id=1, source_target_pairs={{0,32},{32,0},{64,96},{96,64},{128,160},{160,128},{192,224},{224,1... | collective-permute-start | bytes 393224 | tf_op jit(solution)/shard_map/ppermute | solution.py:35
  11.0 2.6 collective-permute-done
  13.6 0.1 copy.10
  13.7 0.1 broadcast_in_dim.21
  13.8 17.0 %all_to_all.46 = f32[8,256,128]{1,2,0:T(8,128)S(1)} all-to-all(f32[8,256,128]{1,2,0:T(8,128)S(1)} %broadcast_in_dim.21), channel_id=1, replica_groups=mesh['box'=16,'row'=4,'col'=8] {'col'}, dimensions={0} | all-to-all | bytes 2097152 | tf_op jit(solution)/shard_map/all_to_all | solution.py:25
  30.8 0.0 copy-done
  30.8 1.2 broadcast_in_dim.29
  32.0 9.1 %all-to-all-start.7 = ((f32[4,256,384]{2,1,0:T(8,128)}), f32[4,256,384]{2,1,0:T(8,128)S(1)}, u32[]{:S(2)}, u32[]{:S(2)}) async-start(f32[4,256,384]{2,1,0:T(8,128)} %broadcast_in_dim.29), calls=%async_computation.7 | async-start | bytes 3145728 | tf_op jit(solution)/shard_map/all_to_all | solution.py:25
  41.1 0.0 all-gather.4.cloned.1.call-start
  41.1 3.2 %collective-permute-start.1 = (f32[256,384]{1,0:T(8,128)S(1)}, f32[256,384]{1,0:T(8,128)S(1)}, u32[]{:S(2)}, u32[]{:S(2)}) collective-permute-start(f32[256,384]{1,0:T(8,128)S(1)} %bitcast.54), channel_id=1, source_target_pairs={{0,32},{32,0},{64,96},{96,64},{128,160},{160,128},{192,224},{224,1... | collective-permute-start | bytes 1179656 | tf_op jit(solution)/shard_map/ppermute | solution.py:35
  44.3 9.4 %collective-permute-done.1 = f32[256,384]{1,0:T(8,128)S(1)} collective-permute-done((f32[256,384]{1,0:T(8,128)S(1)}, f32[256,384]{1,0:T(8,128)S(1)}, u32[]{:S(2)}, u32[]{:S(2)}) %collective-permute-start.1) | collective-permute-done | bytes 393248 | tf_op jit(solution)/shard_map/ppermute | solution.py:35
  53.6 8.0 %all-to-all-done.7 = f32[4,256,384]{2,1,0:T(8,128)S(1)} async-done(((f32[4,256,384]{2,1,0:T(8,128)}), f32[4,256,384]{2,1,0:T(8,128)S(1)}, u32[]{:S(2)}, u32[]{:S(2)}) %all-to-all-start.7) | async-done | bytes 1572896 | tf_op jit(solution)/shard_map/all_to_all | solution.py:25
  61.7 1.9 broadcast_select_fusion.1
  63.5 1.0 pad_maximum_fusion
  64.5 0.0 all-gather.4.cloned.1.call-update
  64.5 0.0 copy-done.1
  64.5 0.8 broadcast_in_dim.22
  65.3 4.4 %all-to-all-start.1 = ((f32[4,256,128]{2,1,0:T(8,128)}), f32[4,256,128]{2,1,0:T(8,128)S(1)}, u32[]{:S(2)}, u32[]{:S(2)}) async-start(f32[4,256,128]{2,1,0:T(8,128)} %broadcast_in_dim.22), calls=%async_computation.1 | async-start | bytes 1048576 | tf_op jit(solution)/shard_map/all_to_all | solution.py:25
  69.8 9.3 %all-to-all-done.1 = f32[4,256,128]{2,1,0:T(8,128)S(1)} async-done(((f32[4,256,128]{2,1,0:T(8,128)}), f32[4,256,128]{2,1,0:T(8,128)S(1)}, u32[]{:S(2)}, u32[]{:S(2)}) %all-to-all-start.1) | async-done | bytes 524320 | tf_op jit(solution)/shard_map/all_to_all | solution.py:25
  79.1 1.8 convert_add_fusion
  80.9 0.8 broadcast_in_dim.25
  81.7 4.4 %all-to-all-start.4 = ((f32[4,256,128]{2,1,0:T(8,128)}), f32[4,256,128]{2,1,0:T(8,128)S(1)}, u32[]{:S(2)}, u32[]{:S(2)}) async-start(f32[4,256,128]{2,1,0:T(8,128)} %broadcast_in_dim.25), calls=%async_computation.4 | async-start | bytes 1048576 | tf_op jit(solution)/shard_map/all_to_all | solution.py:25
  86.2 0.1 copy.12
  86.3 15.5 %all-to-all-done.4 = f32[4,256,128]{2,1,0:T(8,128)S(1)} async-done(((f32[4,256,128]{2,1,0:T(8,128)}), f32[4,256,128]{2,1,0:T(8,128)S(1)}, u32[]{:S(2)}, u32[]{:S(2)}) %all-to-all-start.4) | async-done | bytes 524320 | tf_op jit(solution)/shard_map/all_to_all | solution.py:25
  101.8 1.1 broadcast_in_dim.24
  102.8 3.6 %all-to-all-start.3 = ((f32[8,256,128]{1,2,0:T(8,128)}), f32[8,256,128]{1,2,0:T(8,128)S(1)}, u32[]{:S(2)}, u32[]{:S(2)}) async-start(f32[8,256,128]{1,2,0:T(8,128)} %broadcast_in_dim.24), calls=%async_computation.3 | async-start | bytes 2097152 | tf_op jit(solution)/shard_map/all_to_all | solution.py:25
  106.4 0.0 all-gather.6.cloned.1.call-start
  106.5 0.7 all-gather.6.cloned.1.call-update
  107.2 0.1 copy.11
  107.3 14.7 %all-to-all-done.3 = f32[8,256,128]{1,2,0:T(8,128)S(1)} async-done(((f32[8,256,128]{1,2,0:T(8,128)}), f32[8,256,128]{1,2,0:T(8,128)S(1)}, u32[]{:S(2)}, u32[]{:S(2)}) %all-to-all-start.3) | async-done | bytes 1048608 | tf_op jit(solution)/shard_map/all_to_all | solution.py:25
  122.0 1.1 broadcast_in_dim.23
  123.0 3.6 %all-to-all-start.2 = ((f32[8,256,128]{1,2,0:T(8,128)}), f32[8,256,128]{1,2,0:T(8,128)S(1)}, u32[]{:S(2)}, u32[]{:S(2)}) async-start(f32[8,256,128]{1,2,0:T(8,128)} %broadcast_in_dim.23), calls=%async_computation.2 | async-start | bytes 2097152 | tf_op jit(solution)/shard_map/all_to_all | solution.py:25
  126.6 1.8 fusion.4
  128.4 16.3 %all-to-all-done.2 = f32[8,256,128]{1,2,0:T(8,128)S(1)} async-done(((f32[8,256,128]{1,2,0:T(8,128)}), f32[8,256,128]{1,2,0:T(8,128)S(1)}, u32[]{:S(2)}, u32[]{:S(2)}) %all-to-all-start.2) | async-done | bytes 1048608 | tf_op jit(solution)/shard_map/all_to_all | solution.py:25
  144.7 21.3 %all_to_all.47 = f32[4,256,128]{2,1,0:T(8,128)S(1)} all-to-all(f32[4,256,128]{2,1,0:T(8,128)S(1)} %broadcast_in_dim.26), channel_id=1, replica_groups=mesh['box'=16,'row'=4,'col'=8] {'row'}, dimensions={0} | all-to-all | bytes 1048576 | tf_op jit(solution)/shard_map/all_to_all | solution.py:25
  166.0 1.8 convolution_add_fusion
  167.8 0.1 copy.13
  167.9 0.1 broadcast_in_dim.27
  168.0 29.6 %all_to_all.48 = f32[8,256,128]{1,2,0:T(8,128)S(1)} all-to-all(f32[8,256,128]{1,2,0:T(8,128)S(1)} %broadcast_in_dim.27), channel_id=1, replica_groups=mesh['box'=16,'row'=4,'col'=8] {'col'}, dimensions={0} | all-to-all | bytes 2097152 | tf_op jit(solution)/shard_map/all_to_all | solution.py:25
  197.6 4.7 %fusion.5 = f32[256,768]{1,0:T(8,128)S(1)} fusion(f32[256,1024]{0,1:T(8,128)S(1)} %bitcast.47, f32[1024,768]{1,0:T(8,128)} %all-gather.4.cloned.1.call-done), kind=kOutput, calls=%fused_computation.13 | convolution fusion | flops 2415919104 | bytes 4980736 | tf_op jit(solution)/shard_map/dot_general | solution.py:39
  202.3 1.9 stack.2
  204.2 10.0 %all-to-all-start.8 = ((f32[4,256,768]{2,1,0:T(8,128)}), f32[4,256,768]{2,1,0:T(8,128)S(1)}, u32[]{:S(2)}, u32[]{:S(2)}) async-start(f32[4,256,768]{2,1,0:T(8,128)} %stack.2), calls=%async_computation.8 | async-start | bytes 6291456 | tf_op jit(solution)/shard_map/all_to_all | solution.py:13
  214.3 2.7 copy.8
  216.9 2.8 select_bitcast_fusion.1
  219.7 8.9 %all-gather.6.cloned.1.call-done = f32[1,768,1024]{2,1,0:T(8,128)} async-done(((f32[1,768,128]{2,1,0:T(8,128)}), f32[1,768,1024]{2,1,0:T(8,128)}) %all-gather.6.cloned.1.call-update) | async-done | bytes 3145744 | tf_op jit(solution)/shard_map/all_gather | solution.py:84
  228.7 28.4 %all-to-all-done.8 = f32[4,256,768]{2,1,0:T(8,128)S(1)} async-done(((f32[4,256,768]{2,1,0:T(8,128)}), f32[4,256,768]{2,1,0:T(8,128)S(1)}, u32[]{:S(2)}, u32[]{:S(2)}) %all-to-all-start.8) | async-done | bytes 3145760 | tf_op jit(solution)/shard_map/all_to_all | solution.py:13
  257.0 18.6 %maximum_add_fusion = f32[768,768]{0,1:T(8,128)} fusion(f32[768,384]{0,1:T(8,128)} %get-tuple-element.6, f32[768,384]{0,1:T(8,128)} %get-tuple-element.5, f32[1024,768]{1,0:T(8,128)S(1)} %bitcast.42, f32[1,768,1024]{2,1,0:T(8,128)} %all-gather.6.cloned.1.call-done), kind=kOutput, calls=%fused_computation.2 | convolution fusion | flops 7248936960 | bytes 11010048 | tf_op jit(solution)/shard_map/dot_general | solution.py:39
  275.6 5.3 %copy.14 = f32[1,768,2,384]{3,2,1,0:T(2,128)} copy(f32[1,768,2,384]{1,3,2,0:T(8,128)} %bitcast.43) | data formatting | bytes 4718592 | tf_op jit(solution)/shard_map/reshape | solution.py:85
  (6 shorter events, 0.0 us)
Async XLA Ops:
  6.5 24.2 %copy-start = (f32[1,256,384]{2,1,0:T(8,128)S(1)}, f32[1,256,384]{2,1,0:T(8,128)}, u32[]{:S(2)}) copy-start(f32[1,256,384]{2,1,0:T(8,128)} %param.6) | copy-start | bytes 1179652
  6.5 7.0 %collective-permute-start = (f32[256,128]{1,0:T(8,128)}, f32[256,128]{1,0:T(8,128)S(1)}, u32[]{:S(2)}, u32[]{:S(2)}) collective-permute-start(f32[256,128]{1,0:T(8,128)} %bitcast.55), channel_id=1, source_target_pairs={{0,32},{32,0},{64,96},{96,64},{128,160},{160,128},{192,224},{224,1... | collective-permute-start | bytes 393224 | tf_op jit(solution)/shard_map/ppermute | solution.py:35
  32.0 29.6 %all-to-all-start.7 = ((f32[4,256,384]{2,1,0:T(8,128)}), f32[4,256,384]{2,1,0:T(8,128)S(1)}, u32[]{:S(2)}, u32[]{:S(2)}) async-start(f32[4,256,384]{2,1,0:T(8,128)} %broadcast_in_dim.29), calls=%async_computation.7 | async-start | bytes 3145728 | tf_op jit(solution)/shard_map/all_to_all | solution.py:25
  41.1 156.5 %all-gather.4.cloned.1.call-start = ((), (), s32[]{:S(2)}) async-start(), calls=%async_computation.9 | async-start | bytes 3932160 | tf_op jit(solution)/shard_map/all_gather | solution.py:75
  41.1 12.6 %collective-permute-start.1 = (f32[256,384]{1,0:T(8,128)S(1)}, f32[256,384]{1,0:T(8,128)S(1)}, u32[]{:S(2)}, u32[]{:S(2)}) collective-permute-start(f32[256,384]{1,0:T(8,128)S(1)} %bitcast.54), channel_id=1, source_target_pairs={{0,32},{32,0},{64,96},{96,64},{128,160},{160,128},{192,224},{224,1... | collective-permute-start | bytes 1179656 | tf_op jit(solution)/shard_map/ppermute | solution.py:35
  61.7 2.9 copy-start.1
  65.3 13.8 %all-to-all-start.1 = ((f32[4,256,128]{2,1,0:T(8,128)}), f32[4,256,128]{2,1,0:T(8,128)S(1)}, u32[]{:S(2)}, u32[]{:S(2)}) async-start(f32[4,256,128]{2,1,0:T(8,128)} %broadcast_in_dim.22), calls=%async_computation.1 | async-start | bytes 1048576 | tf_op jit(solution)/shard_map/all_to_all | solution.py:25
  81.7 20.0 %all-to-all-start.4 = ((f32[4,256,128]{2,1,0:T(8,128)}), f32[4,256,128]{2,1,0:T(8,128)S(1)}, u32[]{:S(2)}, u32[]{:S(2)}) async-start(f32[4,256,128]{2,1,0:T(8,128)} %broadcast_in_dim.25), calls=%async_computation.4 | async-start | bytes 1048576 | tf_op jit(solution)/shard_map/all_to_all | solution.py:25
  102.8 19.1 %all-to-all-start.3 = ((f32[8,256,128]{1,2,0:T(8,128)}), f32[8,256,128]{1,2,0:T(8,128)S(1)}, u32[]{:S(2)}, u32[]{:S(2)}) async-start(f32[8,256,128]{1,2,0:T(8,128)} %broadcast_in_dim.24), calls=%async_computation.3 | async-start | bytes 2097152 | tf_op jit(solution)/shard_map/all_to_all | solution.py:25
  106.4 122.3 %all-gather.6.cloned.1.call-start = ((), (), s32[]{:S(2)}) async-start(), calls=%async_computation.10 | async-start | bytes 3538944 | tf_op jit(solution)/shard_map/all_gather | solution.py:84
  123.0 21.7 %all-to-all-start.2 = ((f32[8,256,128]{1,2,0:T(8,128)}), f32[8,256,128]{1,2,0:T(8,128)S(1)}, u32[]{:S(2)}, u32[]{:S(2)}) async-start(f32[8,256,128]{1,2,0:T(8,128)} %broadcast_in_dim.23), calls=%async_computation.2 | async-start | bytes 2097152 | tf_op jit(solution)/shard_map/all_to_all | solution.py:25
  204.2 52.8 %all-to-all-start.8 = ((f32[4,256,768]{2,1,0:T(8,128)}), f32[4,256,768]{2,1,0:T(8,128)S(1)}, u32[]{:S(2)}, u32[]{:S(2)}) async-start(f32[4,256,768]{2,1,0:T(8,128)} %stack.2), calls=%async_computation.8 | async-start | bytes 6291456 | tf_op jit(solution)/shard_map/all_to_all | solution.py:13
Sparse Core Ops, SparseCore 0:
  64.6 53.5 all-gather.3
  120.2 108.4 all-gather.5
